TPU v7x, 128 devices: a whole 4x4x4 slice. The times are simulated.
128 devices in a mesh: section: 4 (over x_lo, core), tok: 32 (over y, z, x_hi).
Axes of the slice: x: 4 (x_hi: 2, x_lo: 2; x = x_hi * 2 + x_lo), y: 4, z: 4, core: 2. Of those that a mesh axis runs over, the one named last changes fastest.
Arguments:
- states: bfloat16 [8, 2048, 4096], P('section', 'tok'), may hold values from -60 to 60
- spans: int32 [2, 2], replicated, may hold values from 0 to 7, as said below
Outputs:
- bridges: float32 [2, 4096, 4096], P(None, 'section', 'tok')
- residuals: float32 [2, 4096, 4096], P(None, 'section', 'tok')
Inputs may be any that keep to these rules, and one draw needn't show every extreme that they name: `spans`: each row is (start, end) with end - start at least 2.
All inputs are finite; a program needn't handle non-finite values.
Results may differ from a plain program's by a relative error of at most 0.0093.
Values may be sent and summed in bfloat16 or wider, within the bound.
A program may use at most 64 MiB of HBM per device.

v0:
```python
import jax
import jax.numpy as jnp
from jax import lax
from jax.sharding import Mesh
from jax.sharding import PartitionSpec as P

CG_STEPS = 2
SECTION = ("section_0", "section_1")
TOK = ("tok_0", "tok_1", "tok_2")
SECTION_TOK = ("section_0", "section_1", "tok_0", "tok_1", "tok_2")
RIDGE = 0.25


def padded_to(lines, devices):
    spare = -lines.shape[0] % devices
    if not spare:
        return lines
    return jnp.concatenate([lines, jnp.zeros((spare, *lines.shape[1:]), lines.dtype)])


def from_root(value, axis, root):
    lines = jnp.where(lax.axis_index(axis) == root, value, jnp.zeros_like(value)).reshape(
        -1, *value.shape[1:][-1:]
    )
    padded = padded_to(lines, lax.axis_size(axis))
    own = lax.psum_scatter(padded, axis, scatter_dimension=0, tiled=True)
    return lax.all_gather(own, axis, axis=0, tiled=True)[: len(lines)].reshape(value.shape)


def in_blocks(value, dim, devices):
    before, after = (value.shape[:dim], value.shape[dim + 1 :])
    return jnp.moveaxis(value.reshape(*before, devices, -1, *after), dim, 0)


def sum_at_owner(value, axis, dim):
    devices = lax.axis_size(axis)
    blocks = lax.all_to_all(in_blocks(value, dim, devices), axis, 0, 0, tiled=True)
    return jnp.sum(blocks, axis=0)


def joined_along(blocks, dim):
    blocks = jnp.moveaxis(blocks, 0, dim)
    lengths = blocks.shape
    return blocks.reshape(*lengths[:dim], lengths[dim] * lengths[dim + 1], *lengths[dim + 2 :])


def copy_for_each(value, axis):
    copies = jnp.broadcast_to(value, (lax.axis_size(axis), *value.shape))
    return lax.all_to_all(copies, axis, split_axis=0, concat_axis=0, tiled=True)


def gather_directly(value, axis, dim):
    return joined_along(copy_for_each(value, axis), dim)


def over_axes(value, axes):
    for axis in axes:
        value = lax.psum(value, axis)
    return value


def transposed(left, right_hand):
    return lax.dot_general(
        left, right_hand, (((0,), (0,)), ((), ())), preferred_element_type=jnp.float32
    )


def conjugate(operators, rights, summed):
    bridges = [jnp.zeros_like(right_side) for right_side in rights]
    residuals = list(rights)
    directions = list(rights)
    squares = summed([jnp.sum(right_side * right_side) for right_side in rights])
    for step in range(CG_STEPS):
        images = [operators[k](directions[k]) for k in range(len(rights))]
        curvatures = summed([jnp.sum(directions[k] * images[k]) for k in range(len(rights))])
        for k in range(len(rights)):
            step_size = squares[k] / curvatures[k]
            bridges[k] = bridges[k] + step_size * directions[k]
            residuals[k] = residuals[k] - step_size * images[k]
        if step + 1 < CG_STEPS:
            renewed = summed([jnp.sum(residual * residual) for residual in residuals])
            for k in range(len(rights)):
                directions[k] = residuals[k] + renewed[k] / squares[k] * directions[k]
            squares = renewed
    return (bridges, residuals)


def per_device(states, spans):
    sections = lax.axis_size(SECTION)
    section_index = lax.axis_index(SECTION)
    tok_count = lax.axis_size(TOK)
    layers_here, tok_rows, feature_width = states.shape
    total_rows = tok_rows * tok_count
    scaling = 1.0 / total_rows
    block_width = feature_width // sections

    def fetch(boundary):
        picked = lax.dynamic_index_in_dim(states, boundary % layers_here, 0, keepdims=False)
        return from_root(picked, SECTION, boundary // layers_here)

    def prepare(k):
        source = fetch(spans[k, 0])
        target = fetch(spans[k, 1])
        target_cols = lax.all_to_all(target, TOK, split_axis=1, concat_axis=0, tiled=True)
        sliced = lax.dynamic_slice_in_dim(source, section_index * block_width, block_width, 1)
        source_cols = lax.all_gather(sliced, TOK, axis=0, tiled=True)
        right_side = transposed(source_cols, target_cols) * scaling

        def operator(direction):
            direction_low = direction.astype(jnp.bfloat16)
            shared = sum_at_owner(
                jnp.dot(source_cols, direction_low, preferred_element_type=jnp.float32), SECTION, 0
            )
            mapped = gather_directly(shared.astype(jnp.bfloat16), SECTION, 0)
            return transposed(source_cols, mapped) * scaling + RIDGE * direction

        return (operator, right_side)

    setups = [prepare(k) for k in range(spans.shape[0])]

    def summed(values):
        totals = over_axes(jnp.stack(values), SECTION_TOK)
        return [totals[k] for k in range(len(values))]

    bridges, residuals = conjugate(
        [entry[0] for entry in setups], [entry[1] for entry in setups], summed
    )
    return (jnp.stack(bridges), jnp.stack(residuals))


def solution(mesh):
    split = Mesh(
        mesh.devices.reshape(2, 2, 4, 4, 2), ("section_0", "section_1", "tok_0", "tok_1", "tok_2")
    )
    return jax.shard_map(
        per_device,
        mesh=split,
        in_specs=(P(SECTION, TOK, None), P()),
        out_specs=(P(None, SECTION, TOK), P(None, SECTION, TOK)),
        check_vma=False,
    )
```

profile of v0, /device:TPU:0, one launch (start us, length us, event | category | flops | bytes accessed | tf_op | source)
XLA Modules:
  0.0 532.0 jit_solution(17612834347519697008)
XLA Ops:
  24.2 18.6 %reduce-scatter.5.cloned.1.call-done = bf16[16,4096]{1,0:T(8,128)(2,1)} async-done(((bf16[64,4096]{1,0:T(8,128)(2,1)}), bf16[16,4096]{1,0:T(8,128)(2,1)}) %reduce-scatter.5.cloned.1.call-update) | async-done | bytes 131088 | tf_op jit(solution)/shard_map/reduce_scatter | solution.py:26
  42.7 7.8 %all_gather.18 = bf16[64,4096]{1,0:T(8,128)(2,1)S(1)} all-gather(bf16[16,4096]{1,0:T(8,128)(2,1)} %reduce-scatter.5.cloned.1.call-done), channel_id=1, replica_groups=mesh['section_0'=2,'section_1'=2,'tok_0'=4,'tok_1'=4,'tok_2'=2] {'sectio..., dimensions={0}, use_global_device_ids=true | all-gather | bytes 655360 | tf_op jit(solution)/shard_map/all_gather | solution.py:27
  51.3 13.2 %reduce-scatter.9.cloned.1.call-done = bf16[16,4096]{1,0:T(8,128)(2,1)} async-done(((bf16[64,4096]{1,0:T(8,128)(2,1)}), bf16[16,4096]{1,0:T(8,128)(2,1)}) %reduce-scatter.9.cloned.1.call-update) | async-done | bytes 131088 | tf_op jit(solution)/shard_map/reduce_scatter | solution.py:26
  64.5 7.8 %all_gather.21 = bf16[64,4096]{1,0:T(8,128)(2,1)S(1)} all-gather(bf16[16,4096]{1,0:T(8,128)(2,1)} %reduce-scatter.9.cloned.1.call-done), channel_id=1, replica_groups=mesh['section_0'=2,'section_1'=2,'tok_0'=4,'tok_1'=4,'tok_2'=2] {'sectio..., dimensions={0}, use_global_device_ids=true | all-gather | bytes 655360 | tf_op jit(solution)/shard_map/all_gather | solution.py:27
  73.0 13.8 %reduce-scatter.7.cloned.1.call-done = bf16[16,4096]{1,0:T(8,128)(2,1)} async-done(((bf16[64,4096]{1,0:T(8,128)(2,1)}), bf16[16,4096]{1,0:T(8,128)(2,1)}) %reduce-scatter.7.cloned.1.call-update) | async-done | bytes 131088 | tf_op jit(solution)/shard_map/reduce_scatter | solution.py:26
  86.8 7.8 %all_gather.20 = bf16[64,4096]{1,0:T(8,128)(2,1)S(1)} all-gather(bf16[16,4096]{1,0:T(8,128)(2,1)} %reduce-scatter.7.cloned.1.call-done), channel_id=1, replica_groups=mesh['section_0'=2,'section_1'=2,'tok_0'=4,'tok_1'=4,'tok_2'=2] {'sectio..., dimensions={0}, use_global_device_ids=true | all-gather | bytes 655360 | tf_op jit(solution)/shard_map/all_gather | solution.py:27
  95.6 9.4 %all-to-all-start = ((bf16[64,32,128]{2,0,1:T(8,128)(2,1)}), bf16[64,32,128]{2,0,1:T(8,128)(2,1)S(1)}, u32[]{:S(2)}, u32[]{:S(2)}) async-start(bf16[64,32,128]{2,0,1:T(8,128)(2,1)} %copy_bitcast_fusion.1), calls=%async_computation.2 | async-start | bytes 1048576 | tf_op jit(solution)/shard_map/all_to_all | solution.py:104
  105.0 4.7 reduce-scatter.11.cloned.1.call-done
  109.7 7.4 %all_gather.23 = bf16[64,4096]{1,0:T(8,128)(2,1)S(1)} all-gather(bf16[16,4096]{1,0:T(8,128)(2,1)} %reduce-scatter.11.cloned.1.call-done), channel_id=1, replica_groups=mesh['section_0'=2,'section_1'=2,'tok_0'=4,'tok_1'=4,'tok_2'=2] {'sectio..., dimensions={0}, use_global_device_ids=true | all-gather | bytes 655360 | tf_op jit(solution)/shard_map/all_gather | solution.py:27
  120.2 7.3 %all-to-all-start.1 = ((bf16[64,32,128]{2,0,1:T(8,128)(2,1)}), bf16[64,32,128]{2,0,1:T(8,128)(2,1)S(1)}, u32[]{:S(2)}, u32[]{:S(2)}) async-start(bf16[64,32,128]{2,0,1:T(8,128)(2,1)} %copy_bitcast_fusion), calls=%async_computation.5 | async-start | bytes 1048576 | tf_op jit(solution)/shard_map/all_to_all | solution.py:104
  127.5 68.5 %all-gather.3.cloned.1.call-done = bf16[2048,1024]{1,0:T(8,128)(2,1)} async-done(((bf16[64,1024]{1,0:T(8,128)(2,1)}), bf16[2048,1024]{1,0:T(8,128)(2,1)}) %all-gather.3.cloned.1.call-update) | async-done | bytes 4194320 | tf_op jit(solution)/shard_map/all_gather | solution.py:106
  205.4 73.2 %all-gather.5.cloned.1.call-done = bf16[2048,1024]{1,0:T(8,128)(2,1)} async-done(((bf16[64,1024]{1,0:T(8,128)(2,1)}), bf16[2048,1024]{1,0:T(8,128)(2,1)}) %all-gather.5.cloned.1.call-update) | async-done | bytes 4194320 | tf_op jit(solution)/shard_map/all_gather | solution.py:106
  288.1 14.3 %all-to-all-done.4 = f32[4,512,128]{2,1,0:T(8,128)S(1)} async-done(((f32[4,512,128]{2,1,0:T(8,128)}), f32[4,512,128]{2,1,0:T(8,128)S(1)}, u32[]{:S(2)}, u32[]{:S(2)}) %all-to-all-start.4) | async-done | bytes 1048608 | tf_op jit(solution)/shard_map/all_to_all | solution.py:37
  306.8 8.7 %all-to-all-done.3 = bf16[4,512,128]{2,1,0:T(8,128)(2,1)S(1)} async-done(((bf16[4,512,128]{2,1,0:T(8,128)(2,1)}), bf16[4,512,128]{2,1,0:T(8,128)(2,1)S(1)}, u32[]{:S(2)}, u32[]{:S(2)}) %all-to-all-start.3) | async-done | bytes 524320 | tf_op jit(solution)/shard_map/all_to_all | solution.py:49
  324.3 4.6 all-to-all-done.5
  335.5 4.9 all-reduce.4
  342.8 10.1 %all-reduce.1 = (f32[2]{0:T(128)S(1)}, f32[2]{0:T(128)S(1)}) all-reduce(f32[2]{0:T(128)S(1)} %get-tuple-element.12, f32[2]{0:T(128)S(1)} %get-tuple-element.13), channel_id=1, replica_groups=mesh['section_0'=2,'section_1'=2,'tok_0'=4,'tok_1'=4,'tok_2'=2] {'tok_0'}, use_global_device_ids=true, to_apply=%region_8.9 | all-reduce | flops 4 | bytes 32 | tf_op jit(solution)/shard_map/psum | solution.py:58
  352.9 10.7 %all-reduce = (f32[2]{0:T(128)S(1)}, f32[2]{0:T(128)S(1)}) all-reduce(f32[2]{0:T(128)S(1)} %get-tuple-element.8, f32[2]{0:T(128)S(1)} %get-tuple-element.9), channel_id=1, replica_groups=mesh['section_0'=2,'section_1'=2,'tok_0'=4,'tok_1'=4,'tok_2'=2] {'tok_1'}, use_global_device_ids=true, to_apply=%region_9.10 | all-reduce | flops 4 | bytes 32 | tf_op jit(solution)/shard_map/psum | solution.py:58
  363.6 6.6 %all-reduce.2 = (f32[2]{0:T(128)S(1)}, f32[2]{0:T(128)S(1)}) all-reduce(f32[2]{0:T(128)S(1)} %get-tuple-element.6, f32[2]{0:T(128)S(1)} %get-tuple-element.7), channel_id=1, replica_groups=mesh['section_0'=2,'section_1'=2,'tok_0'=4,'tok_1'=4,'tok_2'=2] {'tok_2'}, use_global_device_ids=true, to_apply=%region_10.11 | all-reduce | flops 4 | bytes 32 | tf_op jit(solution)/shard_map/psum | solution.py:58
  377.1 4.9 psum.150
  384.4 7.7 %psum.152 = f32[2]{0:T(128)S(1)} all-reduce(f32[2]{0:T(128)S(1)} %psum.151), channel_id=1, replica_groups=mesh['section_0'=2,'section_1'=2,'tok_0'=4,'tok_1'=4,'tok_2'=2] {'tok_0'}, use_global_device_ids=true, to_apply=%region_24.25 | all-reduce | flops 2 | bytes 16 | tf_op jit(solution)/shard_map/psum | solution.py:58
  392.1 7.7 %psum.153 = f32[2]{0:T(128)S(1)} all-reduce(f32[2]{0:T(128)S(1)} %psum.152), channel_id=1, replica_groups=mesh['section_0'=2,'section_1'=2,'tok_0'=4,'tok_1'=4,'tok_2'=2] {'tok_1'}, use_global_device_ids=true, to_apply=%region_25.26 | all-reduce | flops 2 | bytes 16 | tf_op jit(solution)/shard_map/psum | solution.py:58
  399.8 6.4 %psum.154 = f32[2]{0:T(128)S(1)} all-reduce(f32[2]{0:T(128)S(1)} %psum.153), channel_id=1, replica_groups=mesh['section_0'=2,'section_1'=2,'tok_0'=4,'tok_1'=4,'tok_2'=2] {'tok_2'}, use_global_device_ids=true, to_apply=%region_26.27 | all-reduce | flops 2 | bytes 16 | tf_op jit(solution)/shard_map/psum | solution.py:58
  422.8 8.6 %all-to-all-done.6 = f32[4,512,128]{2,1,0:T(8,128)} async-done(((f32[4,512,128]{2,1,0:T(8,128)}), f32[4,512,128]{2,1,0:T(8,128)}, u32[]{:S(2)}, u32[]{:S(2)}) %all-to-all-start.6) | async-done | bytes 1048608 | tf_op jit(solution)/shard_map/all_to_all | solution.py:37
  437.0 13.2 %all-to-all-done.8 = f32[4,512,128]{2,1,0:T(8,128)} async-done(((f32[4,512,128]{2,1,0:T(8,128)}), f32[4,512,128]{2,1,0:T(8,128)}, u32[]{:S(2)}, u32[]{:S(2)}) %all-to-all-start.8) | async-done | bytes 1048608 | tf_op jit(solution)/shard_map/all_to_all | solution.py:37
  456.5 7.6 %all-to-all-done.7 = bf16[4,512,128]{2,1,0:T(8,128)(2,1)} async-done(((bf16[4,512,128]{2,1,0:T(8,128)(2,1)}), bf16[4,512,128]{2,1,0:T(8,128)(2,1)}, u32[]{:S(2)}, u32[]{:S(2)}) %all-to-all-start.7) | async-done | bytes 524320 | tf_op jit(solution)/shard_map/all_to_all | solution.py:49
  469.1 5.0 multiply_reduce_fusion.1
  478.0 5.0 multiply_reduce_fusion
  484.3 4.9 psum.155
  491.7 9.7 %psum.157 = f32[2]{0:T(128)S(1)} all-reduce(f32[2]{0:T(128)S(1)} %psum.156), channel_id=1, replica_groups=mesh['section_0'=2,'section_1'=2,'tok_0'=4,'tok_1'=4,'tok_2'=2] {'tok_0'}, use_global_device_ids=true, to_apply=%region_33.34 | all-reduce | flops 2 | bytes 16 | tf_op jit(solution)/shard_map/psum | solution.py:58
  501.4 9.7 %psum.158 = f32[2]{0:T(128)S(1)} all-reduce(f32[2]{0:T(128)S(1)} %psum.157), channel_id=1, replica_groups=mesh['section_0'=2,'section_1'=2,'tok_0'=4,'tok_1'=4,'tok_2'=2] {'tok_1'}, use_global_device_ids=true, to_apply=%region_34.35 | all-reduce | flops 2 | bytes 16 | tf_op jit(solution)/shard_map/psum | solution.py:58
  511.1 6.4 %psum.159 = f32[2]{0:T(128)S(1)} all-reduce(f32[2]{0:T(128)S(1)} %psum.158), channel_id=1, replica_groups=mesh['section_0'=2,'section_1'=2,'tok_0'=4,'tok_1'=4,'tok_2'=2] {'tok_2'}, use_global_device_ids=true, to_apply=%region_35.36 | all-reduce | flops 2 | bytes 16 | tf_op jit(solution)/shard_map/psum | solution.py:58
  (70 shorter events, 103.1 us)
Async XLA Ops:
  7.2 35.6 %reduce-scatter.5.cloned.1.call-start = ((), (), s32[]{:S(2)}) async-start(), calls=%async_computation.14 | async-start | bytes 655360 | tf_op jit(solution)/shard_map/reduce_scatter | solution.py:26
  22.1 42.4 %reduce-scatter.9.cloned.1.call-start = ((), (), s32[]{:S(2)}) async-start(), calls=%async_computation.17 | async-start | bytes 655360 | tf_op jit(solution)/shard_map/reduce_scatter | solution.py:26
  22.8 64.0 %reduce-scatter.7.cloned.1.call-start = ((), (), s32[]{:S(2)}) async-start(), calls=%async_computation.16 | async-start | bytes 655360 | tf_op jit(solution)/shard_map/reduce_scatter | solution.py:26
  23.5 86.1 %reduce-scatter.11.cloned.1.call-start = ((), (), s32[]{:S(2)}) async-start(), calls=%async_computation.19 | async-start | bytes 655360 | tf_op jit(solution)/shard_map/reduce_scatter | solution.py:26
  24.1 171.9 %all-gather.3.cloned.1.call-start = ((), (), s32[]{:S(2)}) async-start(), calls=%async_computation.15 | async-start | bytes 4325376 | tf_op jit(solution)/shard_map/all_gather | solution.py:106
  51.3 227.4 %all-gather.5.cloned.1.call-start = ((), (), s32[]{:S(2)}) async-start(), calls=%async_computation.18 | async-start | bytes 4325376 | tf_op jit(solution)/shard_map/all_gather | solution.py:106
  95.6 24.6 %all-to-all-start = ((bf16[64,32,128]{2,0,1:T(8,128)(2,1)}), bf16[64,32,128]{2,0,1:T(8,128)(2,1)S(1)}, u32[]{:S(2)}, u32[]{:S(2)}) async-start(bf16[64,32,128]{2,0,1:T(8,128)(2,1)} %copy_bitcast_fusion.1), calls=%async_computation.2 | async-start | bytes 1048576 | tf_op jit(solution)/shard_map/all_to_all | solution.py:104
  120.2 81.7 %all-to-all-start.1 = ((bf16[64,32,128]{2,0,1:T(8,128)(2,1)}), bf16[64,32,128]{2,0,1:T(8,128)(2,1)S(1)}, u32[]{:S(2)}, u32[]{:S(2)}) async-start(bf16[64,32,128]{2,0,1:T(8,128)(2,1)} %copy_bitcast_fusion), calls=%async_computation.5 | async-start | bytes 1048576 | tf_op jit(solution)/shard_map/all_to_all | solution.py:104
  196.0 3.6 copy-start
  201.9 82.6 %all-to-all-start.2 = ((f32[4,512,128]{2,1,0:T(8,128)}), f32[4,512,128]{2,1,0:T(8,128)S(1)}, u32[]{:S(2)}, u32[]{:S(2)}) async-start(f32[4,512,128]{2,1,0:T(8,128)} %bitcast.14), calls=%async_computation.6 | async-start | bytes 2097152 | tf_op jit(solution)/shard_map/all_to_all | solution.py:37
  278.6 3.6 copy-start.1
  284.5 17.9 %all-to-all-start.4 = ((f32[4,512,128]{2,1,0:T(8,128)}), f32[4,512,128]{2,1,0:T(8,128)S(1)}, u32[]{:S(2)}, u32[]{:S(2)}) async-start(f32[4,512,128]{2,1,0:T(8,128)} %bitcast.17), calls=%async_computation.8 | async-start | bytes 2097152 | tf_op jit(solution)/shard_map/all_to_all | solution.py:37
  303.3 12.3 %all-to-all-start.3 = ((bf16[4,512,128]{2,1,0:T(8,128)(2,1)}), bf16[4,512,128]{2,1,0:T(8,128)(2,1)S(1)}, u32[]{:S(2)}, u32[]{:S(2)}) async-start(bf16[4,512,128]{2,1,0:T(8,128)(2,1)} %broadcast_in_dim.12), calls=%async_computation.7 | async-start | bytes 1048576 | tf_op jit(solution)/shard_map/all_to_all | solution.py:49
  315.5 4.5 copy-start.2
  316.6 12.3 %all-to-all-start.5 = ((bf16[4,512,128]{2,1,0:T(8,128)(2,1)}), bf16[4,512,128]{2,1,0:T(8,128)(2,1)S(1)}, u32[]{:S(2)}, u32[]{:S(2)}) async-start(bf16[4,512,128]{2,1,0:T(8,128)(2,1)} %broadcast_in_dim.13), calls=%async_computation.9 | async-start | bytes 1048576 | tf_op jit(solution)/shard_map/all_to_all | solution.py:49
  412.7 18.8 %all-to-all-start.6 = ((f32[4,512,128]{2,1,0:T(8,128)}), f32[4,512,128]{2,1,0:T(8,128)}, u32[]{:S(2)}, u32[]{:S(2)}) async-start(f32[4,512,128]{2,1,0:T(8,128)} %bitcast.25), calls=%async_computation.10 | async-start | bytes 2097152 | tf_op jit(solution)/shard_map/all_to_all | solution.py:37
  431.5 18.8 %all-to-all-start.8 = ((f32[4,512,128]{2,1,0:T(8,128)}), f32[4,512,128]{2,1,0:T(8,128)}, u32[]{:S(2)}, u32[]{:S(2)}) async-start(f32[4,512,128]{2,1,0:T(8,128)} %bitcast.29), calls=%async_computation.12 | async-start | bytes 2097152 | tf_op jit(solution)/shard_map/all_to_all | solution.py:37
  451.1 13.0 %all-to-all-start.7 = ((bf16[4,512,128]{2,1,0:T(8,128)(2,1)}), bf16[4,512,128]{2,1,0:T(8,128)(2,1)}, u32[]{:S(2)}, u32[]{:S(2)}) async-start(bf16[4,512,128]{2,1,0:T(8,128)(2,1)} %broadcast_in_dim.14), calls=%async_computation.11 | async-start | bytes 1048576 | tf_op jit(solution)/shard_map/all_to_all | solution.py:49
  465.0 13.0 %all-to-all-start.9 = ((bf16[4,512,128]{2,1,0:T(8,128)(2,1)}), bf16[4,512,128]{2,1,0:T(8,128)(2,1)}, u32[]{:S(2)}, u32[]{:S(2)}) async-start(bf16[4,512,128]{2,1,0:T(8,128)(2,1)} %broadcast_in_dim.15), calls=%async_computation.13 | async-start | bytes 1048576 | tf_op jit(solution)/shard_map/all_to_all | solution.py:49
Sparse Core Ops, SparseCore 0:
  22.2 20.5 reduce-scatter.4
  45.1 19.3 reduce-scatter.8
  67.5 19.3 reduce-scatter.6
  89.1 20.5 reduce-scatter.10
  112.6 83.3 all-gather.2
  198.9 79.6 all-gather.4
where the time goes:
time: 534 us; the launch traced here: 532 us
  waiting for transfers between devices  257 us (48%)
  blocking collectives  128 us (24%)
  starting transfers between devices  47.7 us (9%)
  matrix products  38.9 us (7%)
  between operations  32.5 us (6%)
  other arithmetic  17.1 us (3%)
  local copies, waits for them, and re-layouts  10.8 us (2%)
    all_gather x2, waiting for transfers between devices, prepare(): source_cols = lax.all_gather(sliced, TOK, axis=0, tiled=True)  142 us
    psum x15, blocking collectives, over_axes(): value = lax.psum(value, axis)  97.1 us
    reduce_scatter x4, waiting for transfers between devices, from_root(): own = lax.psum_scatter(padded, axis, scatter_dimension=0, tiled=True)  50.3 us
    all_to_all x4, waiting for transfers between devices, sum_at_owner(): lax.all_to_all(in_blocks(value, dim, devices), axis, 0, 0, tiled=True)  36.2 us
    all_gather x4, blocking collectives, from_root(): lax.all_gather(own, axis, axis=0, tiled=True)[:len(lines)]  30.9 us
    dot_general x6, matrix products, transposed(): lax.dot_general(left, right_hand, (((0,), (0,)), ((), ())), preferred_ele...  25.5 us
    all_to_all x4, waiting for transfers between devices, copy_for_each(): return lax.all_to_all(copies, axis, split_axis=0, concat_axis=0, tiled=True)  24.7 us
    all_to_all x2, starting transfers between devices, prepare(): lax.all_to_all(target, TOK, split_axis=1, concat_axis=0, tiled=True)  16.7 us
  transfers between devices with their start and end apart: 16, of which 14 were waited for; matrix products, arithmetic and copies ran while one was open for 6% of the time, Pallas kernels for 0%

commit v1 on v0

--- a/solution.py
+++ b/solution.py
@@ -103,7 +103,15 @@
         target = fetch(spans[k, 1])
         target_cols = lax.all_to_all(target, TOK, split_axis=1, concat_axis=0, tiled=True)
         sliced = lax.dynamic_slice_in_dim(source, section_index * block_width, block_width, 1)
-        source_cols = lax.all_gather(sliced, TOK, axis=0, tiled=True)
+        source_cols = jnp.concatenate(
+            lax.all_to_all(
+                jnp.stack([sliced for _ in range(lax.axis_size(TOK))], 0),
+                axis_name=TOK,
+                split_axis=0,
+                concat_axis=0,
+            ),
+            0,
+        )
         right_side = transposed(source_cols, target_cols) * scaling
 
         def operator(direction):

time: 534 us -> 513 us (0.961)
  waiting for transfers between devices: 257 us -> 192 us
  starting transfers between devices: 47.7 us -> 67 us
  blocking collectives: 128 us -> 146 us
    all_gather x2 -> x0, waiting for transfers between devices: 142 us -> none  [prepare(): source_cols = lax.all_gather(sliced, TOK, axis=0, tiled=True)]
    all_to_all x0 -> x2, waiting for transfers between devices: none -> 64.7 us  [prepare(): lax.all_to_all(jnp.stack([sliced for _ in range(lax.axis_size(TOK))], 0),...]
    all_gather x4, blocking collectives: 30.9 us -> 53.6 us  [from_root(): lax.all_gather(own, axis, axis=0, tiled=True)[:len(lines)]]
    all_to_all x0 -> x2, starting transfers between devices: none -> 19 us  [prepare(): lax.all_to_all(jnp.stack([sliced for _ in range(lax.axis_size(TOK))], 0),...]
    all_to_all x4, waiting for transfers between devices: 36.2 us -> 42.7 us  [sum_at_owner(): lax.all_to_all(in_blocks(value, dim, devices), axis, 0, 0, tiled=True)]
  transfers between devices with their start and end apart: 16 -> 16, of which waited for: 14 -> 16; matrix products, arithmetic and copies ran while one was open for 6% -> 7% of each run, Pallas kernels for 0% -> 0%
where the time goes in v1:
time: 513 us; the launch traced here: 511 us
  waiting for transfers between devices  192 us (37%)
  blocking collectives  146 us (28%)
  starting transfers between devices  67 us (13%)
  matrix products  42.8 us (8%)
  between operations  32 us (6%)
  other arithmetic  17.1 us (3%)
  local copies, waits for them, and re-layouts  14.2 us (3%)
    psum x15, blocking collectives, over_axes(): value = lax.psum(value, axis)  92.7 us
    all_to_all x2, waiting for transfers between devices, prepare(): lax.all_to_all(jnp.stack([sliced for _ in range(lax.axis_size(TOK))], 0),...  64.7 us
    reduce_scatter x4, waiting for transfers between devices, from_root(): own = lax.psum_scatter(padded, axis, scatter_dimension=0, tiled=True)  53.9 us
    all_gather x4, blocking collectives, from_root(): lax.all_gather(own, axis, axis=0, tiled=True)[:len(lines)]  53.6 us
    all_to_all x4, waiting for transfers between devices, sum_at_owner(): lax.all_to_all(in_blocks(value, dim, devices), axis, 0, 0, tiled=True)  42.7 us
    dot_general x6, matrix products, transposed(): lax.dot_general(left, right_hand, (((0,), (0,)), ((), ())), preferred_ele...  25.1 us
    all_to_all x4, waiting for transfers between devices, copy_for_each(): return lax.all_to_all(copies, axis, split_axis=0, concat_axis=0, tiled=True)  24.7 us
    all_to_all x2, starting transfers between devices, prepare(): lax.all_to_all(jnp.stack([sliced for _ in range(lax.axis_size(TOK))], 0),...  19 us
  transfers between devices with their start and end apart: 16, of which 16 were waited for; matrix products, arithmetic and copies ran while one was open for 7% of the time, Pallas kernels for 0%

profile of v1, /device:TPU:0, one launch (start us, length us, event | category | flops | bytes accessed | tf_op | source)
XLA Modules:
  0.0 511.1 jit_solution(4433740656825645311)
XLA Ops:
  23.7 19.2 %reduce-scatter.11.cloned.1.call-done = bf16[16,4096]{1,0:T(8,128)(2,1)} async-done(((bf16[64,4096]{1,0:T(8,128)(2,1)}), bf16[16,4096]{1,0:T(8,128)(2,1)}) %reduce-scatter.11.cloned.1.call-update) | async-done | bytes 131088 | tf_op jit(solution)/shard_map/reduce_scatter | solution.py:26
  42.9 7.8 %all_gather.15 = bf16[64,4096]{1,0:T(8,128)(2,1)S(1)} all-gather(bf16[16,4096]{1,0:T(8,128)(2,1)} %reduce-scatter.11.cloned.1.call-done), channel_id=1, replica_groups=mesh['section_0'=2,'section_1'=2,'tok_0'=4,'tok_1'=4,'tok_2'=2] {'sectio..., dimensions={0}, use_global_device_ids=true | all-gather | bytes 655360 | tf_op jit(solution)/shard_map/all_gather | solution.py:27
  51.6 9.3 %all-to-all-start.3 = ((bf16[64,32,128]{2,0,1:T(8,128)(2,1)}), bf16[64,32,128]{2,0,1:T(8,128)(2,1)S(1)}, u32[]{:S(2)}, u32[]{:S(2)}) async-start(bf16[64,32,128]{2,0,1:T(8,128)(2,1)} %copy_bitcast_fusion), calls=%async_computation.7 | async-start | bytes 1048576 | tf_op jit(solution)/shard_map/all_to_all | solution.py:104
  61.0 5.6 %reduce-scatter.7.cloned.1.call-done = bf16[16,4096]{1,0:T(8,128)(2,1)} async-done(((bf16[64,4096]{1,0:T(8,128)(2,1)}), bf16[16,4096]{1,0:T(8,128)(2,1)}) %reduce-scatter.7.cloned.1.call-update) | async-done | bytes 131088 | tf_op jit(solution)/shard_map/reduce_scatter | solution.py:26
  66.6 7.5 %all_gather.13 = bf16[64,4096]{1,0:T(8,128)(2,1)S(1)} all-gather(bf16[16,4096]{1,0:T(8,128)(2,1)} %reduce-scatter.7.cloned.1.call-done), channel_id=1, replica_groups=mesh['section_0'=2,'section_1'=2,'tok_0'=4,'tok_1'=4,'tok_2'=2] {'sectio..., dimensions={0}, use_global_device_ids=true | all-gather | bytes 655360 | tf_op jit(solution)/shard_map/all_gather | solution.py:27
  76.5 7.6 %all-to-all-start.1 = ((bf16[64,32,128]{2,0,1:T(8,128)(2,1)}), bf16[64,32,128]{2,0,1:T(8,128)(2,1)S(1)}, u32[]{:S(2)}, u32[]{:S(2)}) async-start(bf16[64,32,128]{2,0,1:T(8,128)(2,1)} %copy_bitcast_fusion.1), calls=%async_computation.3 | async-start | bytes 1048576 | tf_op jit(solution)/shard_map/all_to_all | solution.py:104
  84.1 5.5 %reduce-scatter.5.cloned.1.call-done = bf16[16,4096]{1,0:T(8,128)(2,1)} async-done(((bf16[64,4096]{1,0:T(8,128)(2,1)}), bf16[16,4096]{1,0:T(8,128)(2,1)}) %reduce-scatter.5.cloned.1.call-update) | async-done | bytes 131088 | tf_op jit(solution)/shard_map/reduce_scatter | solution.py:26
  89.6 7.5 %all_gather.12 = bf16[64,4096]{1,0:T(8,128)(2,1)S(1)} all-gather(bf16[16,4096]{1,0:T(8,128)(2,1)} %reduce-scatter.5.cloned.1.call-done), channel_id=1, replica_groups=mesh['section_0'=2,'section_1'=2,'tok_0'=4,'tok_1'=4,'tok_2'=2] {'sectio..., dimensions={0}, use_global_device_ids=true | all-gather | bytes 655360 | tf_op jit(solution)/shard_map/all_gather | solution.py:27
  102.0 6.9 %all-to-all-start = ((bf16[32,64,1024]{2,1,0:T(8,128)(2,1)}), bf16[32,64,1024]{2,1,0:T(8,128)(2,1)}, u32[]{:S(2)}, u32[]{:S(2)}) async-start(bf16[32,64,1024]{2,1,0:T(8,128)(2,1)} %stack.40), calls=%async_computation.1 | async-start | bytes 8388608 | tf_op jit(solution)/shard_map/all_to_all | solution.py:107
  109.5 23.6 %reduce-scatter.9.cloned.1.call-done = bf16[16,4096]{1,0:T(8,128)(2,1)} async-done(((bf16[64,4096]{1,0:T(8,128)(2,1)}), bf16[16,4096]{1,0:T(8,128)(2,1)}) %reduce-scatter.9.cloned.1.call-update) | async-done | bytes 131088 | tf_op jit(solution)/shard_map/reduce_scatter | solution.py:26
  133.1 30.7 %all_gather.14 = bf16[64,4096]{1,0:T(8,128)(2,1)S(1)} all-gather(bf16[16,4096]{1,0:T(8,128)(2,1)} %reduce-scatter.9.cloned.1.call-done), channel_id=1, replica_groups=mesh['section_0'=2,'section_1'=2,'tok_0'=4,'tok_1'=4,'tok_2'=2] {'sectio..., dimensions={0}, use_global_device_ids=true | all-gather | bytes 655360 | tf_op jit(solution)/shard_map/all_gather | solution.py:27
  163.8 8.5 %all-to-all-done = bf16[32,64,1024]{2,1,0:T(8,128)(2,1)} async-done(((bf16[32,64,1024]{2,1,0:T(8,128)(2,1)}), bf16[32,64,1024]{2,1,0:T(8,128)(2,1)}, u32[]{:S(2)}, u32[]{:S(2)}) %all-to-all-start) | async-done | bytes 4194336 | tf_op jit(solution)/shard_map/all_to_all | solution.py:107
  174.8 12.1 %all-to-all-start.2 = ((bf16[32,64,1024]{2,1,0:T(8,128)(2,1)}), bf16[32,64,1024]{2,1,0:T(8,128)(2,1)}, u32[]{:S(2)}, u32[]{:S(2)}) async-start(bf16[32,64,1024]{2,1,0:T(8,128)(2,1)} %stack.42), calls=%async_computation.5 | async-start | bytes 8388608 | tf_op jit(solution)/shard_map/all_to_all | solution.py:107
  194.7 56.2 %all-to-all-done.2 = bf16[32,64,1024]{2,1,0:T(8,128)(2,1)} async-done(((bf16[32,64,1024]{2,1,0:T(8,128)(2,1)}), bf16[32,64,1024]{2,1,0:T(8,128)(2,1)}, u32[]{:S(2)}, u32[]{:S(2)}) %all-to-all-start.2) | async-done | bytes 4194336 | tf_op jit(solution)/shard_map/all_to_all | solution.py:107
  262.3 6.5 %all-to-all-done.4 = f32[4,512,128]{2,1,0:T(8,128)S(1)} async-done(((f32[4,512,128]{2,1,0:T(8,128)}), f32[4,512,128]{2,1,0:T(8,128)S(1)}, u32[]{:S(2)}, u32[]{:S(2)}) %all-to-all-start.4) | async-done | bytes 1048608 | tf_op jit(solution)/shard_map/all_to_all | solution.py:37
  272.4 14.3 %all-to-all-done.6 = f32[4,512,128]{2,1,0:T(8,128)S(1)} async-done(((f32[4,512,128]{2,1,0:T(8,128)}), f32[4,512,128]{2,1,0:T(8,128)S(1)}, u32[]{:S(2)}, u32[]{:S(2)}) %all-to-all-start.6) | async-done | bytes 1048608 | tf_op jit(solution)/shard_map/all_to_all | solution.py:37
  291.2 8.7 %all-to-all-done.5 = bf16[4,512,128]{2,1,0:T(8,128)(2,1)S(1)} async-done(((bf16[4,512,128]{2,1,0:T(8,128)(2,1)}), bf16[4,512,128]{2,1,0:T(8,128)(2,1)S(1)}, u32[]{:S(2)}, u32[]{:S(2)}) %all-to-all-start.5) | async-done | bytes 524320 | tf_op jit(solution)/shard_map/all_to_all | solution.py:49
  319.7 4.9 all-reduce.4
  327.0 7.8 %all-reduce.1 = (f32[2]{0:T(128)S(1)}, f32[2]{0:T(128)S(1)}) all-reduce(f32[2]{0:T(128)S(1)} %get-tuple-element.12, f32[2]{0:T(128)S(1)} %get-tuple-element.13), channel_id=1, replica_groups=mesh['section_0'=2,'section_1'=2,'tok_0'=4,'tok_1'=4,'tok_2'=2] {'tok_0'}, use_global_device_ids=true, to_apply=%region_8.9 | all-reduce | flops 4 | bytes 32 | tf_op jit(solution)/shard_map/psum | solution.py:58
  334.9 8.7 %all-reduce = (f32[2]{0:T(128)S(1)}, f32[2]{0:T(128)S(1)}) all-reduce(f32[2]{0:T(128)S(1)} %get-tuple-element.8, f32[2]{0:T(128)S(1)} %get-tuple-element.9), channel_id=1, replica_groups=mesh['section_0'=2,'section_1'=2,'tok_0'=4,'tok_1'=4,'tok_2'=2] {'tok_1'}, use_global_device_ids=true, to_apply=%region_9.10 | all-reduce | flops 4 | bytes 32 | tf_op jit(solution)/shard_map/psum | solution.py:58
  343.6 6.4 %all-reduce.2 = (f32[2]{0:T(128)S(1)}, f32[2]{0:T(128)S(1)}) all-reduce(f32[2]{0:T(128)S(1)} %get-tuple-element.6, f32[2]{0:T(128)S(1)} %get-tuple-element.7), channel_id=1, replica_groups=mesh['section_0'=2,'section_1'=2,'tok_0'=4,'tok_1'=4,'tok_2'=2] {'tok_2'}, use_global_device_ids=true, to_apply=%region_10.11 | all-reduce | flops 4 | bytes 32 | tf_op jit(solution)/shard_map/psum | solution.py:58
  363.8 9.7 %psum.152 = f32[2]{0:T(128)S(1)} all-reduce(f32[2]{0:T(128)S(1)} %psum.151), channel_id=1, replica_groups=mesh['section_0'=2,'section_1'=2,'tok_0'=4,'tok_1'=4,'tok_2'=2] {'tok_0'}, use_global_device_ids=true, to_apply=%region_24.25 | all-reduce | flops 2 | bytes 16 | tf_op jit(solution)/shard_map/psum | solution.py:58
  373.5 8.6 %psum.153 = f32[2]{0:T(128)S(1)} all-reduce(f32[2]{0:T(128)S(1)} %psum.152), channel_id=1, replica_groups=mesh['section_0'=2,'section_1'=2,'tok_0'=4,'tok_1'=4,'tok_2'=2] {'tok_1'}, use_global_device_ids=true, to_apply=%region_25.26 | all-reduce | flops 2 | bytes 16 | tf_op jit(solution)/shard_map/psum | solution.py:58
  382.2 6.4 %psum.154 = f32[2]{0:T(128)S(1)} all-reduce(f32[2]{0:T(128)S(1)} %psum.153), channel_id=1, replica_groups=mesh['section_0'=2,'section_1'=2,'tok_0'=4,'tok_1'=4,'tok_2'=2] {'tok_2'}, use_global_device_ids=true, to_apply=%region_26.27 | all-reduce | flops 2 | bytes 16 | tf_op jit(solution)/shard_map/psum | solution.py:58
  405.1 8.6 %all-to-all-done.10 = f32[4,512,128]{2,1,0:T(8,128)} async-done(((f32[4,512,128]{2,1,0:T(8,128)}), f32[4,512,128]{2,1,0:T(8,128)}, u32[]{:S(2)}, u32[]{:S(2)}) %all-to-all-start.10) | async-done | bytes 1048608 | tf_op jit(solution)/shard_map/all_to_all | solution.py:37
  419.3 13.2 %all-to-all-done.8 = f32[4,512,128]{2,1,0:T(8,128)} async-done(((f32[4,512,128]{2,1,0:T(8,128)}), f32[4,512,128]{2,1,0:T(8,128)}, u32[]{:S(2)}, u32[]{:S(2)}) %all-to-all-start.8) | async-done | bytes 1048608 | tf_op jit(solution)/shard_map/all_to_all | solution.py:37
  438.8 7.6 %all-to-all-done.11 = bf16[4,512,128]{2,1,0:T(8,128)(2,1)} async-done(((bf16[4,512,128]{2,1,0:T(8,128)(2,1)}), bf16[4,512,128]{2,1,0:T(8,128)(2,1)}, u32[]{:S(2)}, u32[]{:S(2)}) %all-to-all-start.11) | async-done | bytes 524320 | tf_op jit(solution)/shard_map/all_to_all | solution.py:49
  451.4 5.0 multiply_reduce_fusion
  460.3 5.0 multiply_reduce_fusion.1
  474.0 7.8 %psum.157 = f32[2]{0:T(128)S(1)} all-reduce(f32[2]{0:T(128)S(1)} %psum.156), channel_id=1, replica_groups=mesh['section_0'=2,'section_1'=2,'tok_0'=4,'tok_1'=4,'tok_2'=2] {'tok_0'}, use_global_device_ids=true, to_apply=%region_33.34 | all-reduce | flops 2 | bytes 16 | tf_op jit(solution)/shard_map/psum | solution.py:58
  481.8 8.7 %psum.158 = f32[2]{0:T(128)S(1)} all-reduce(f32[2]{0:T(128)S(1)} %psum.157), channel_id=1, replica_groups=mesh['section_0'=2,'section_1'=2,'tok_0'=4,'tok_1'=4,'tok_2'=2] {'tok_1'}, use_global_device_ids=true, to_apply=%region_34.35 | all-reduce | flops 2 | bytes 16 | tf_op jit(solution)/shard_map/psum | solution.py:58
  490.5 6.4 %psum.159 = f32[2]{0:T(128)S(1)} all-reduce(f32[2]{0:T(128)S(1)} %psum.158), channel_id=1, replica_groups=mesh['section_0'=2,'section_1'=2,'tok_0'=4,'tok_1'=4,'tok_2'=2] {'tok_2'}, use_global_device_ids=true, to_apply=%region_35.36 | all-reduce | flops 2 | bytes 16 | tf_op jit(solution)/shard_map/psum | solution.py:58
  (64 shorter events, 126.4 us)
Async XLA Ops:
  7.2 35.7 %reduce-scatter.11.cloned.1.call-start = ((), (), s32[]{:S(2)}) async-start(), calls=%async_computation.19 | async-start | bytes 655360 | tf_op jit(solution)/shard_map/reduce_scatter | solution.py:26
  22.2 44.4 %reduce-scatter.7.cloned.1.call-start = ((), (), s32[]{:S(2)}) async-start(), calls=%async_computation.17 | async-start | bytes 655360 | tf_op jit(solution)/shard_map/reduce_scatter | solution.py:26
  22.9 66.7 %reduce-scatter.5.cloned.1.call-start = ((), (), s32[]{:S(2)}) async-start(), calls=%async_computation.16 | async-start | bytes 655360 | tf_op jit(solution)/shard_map/reduce_scatter | solution.py:26
  51.6 24.8 %all-to-all-start.3 = ((bf16[64,32,128]{2,0,1:T(8,128)(2,1)}), bf16[64,32,128]{2,0,1:T(8,128)(2,1)S(1)}, u32[]{:S(2)}, u32[]{:S(2)}) async-start(bf16[64,32,128]{2,0,1:T(8,128)(2,1)} %copy_bitcast_fusion), calls=%async_computation.7 | async-start | bytes 1048576 | tf_op jit(solution)/shard_map/all_to_all | solution.py:104
  76.5 23.1 %all-to-all-start.1 = ((bf16[64,32,128]{2,0,1:T(8,128)(2,1)}), bf16[64,32,128]{2,0,1:T(8,128)(2,1)S(1)}, u32[]{:S(2)}, u32[]{:S(2)}) async-start(bf16[64,32,128]{2,0,1:T(8,128)(2,1)} %copy_bitcast_fusion.1), calls=%async_computation.3 | async-start | bytes 1048576 | tf_op jit(solution)/shard_map/all_to_all | solution.py:104
  102.0 70.2 %all-to-all-start = ((bf16[32,64,1024]{2,1,0:T(8,128)(2,1)}), bf16[32,64,1024]{2,1,0:T(8,128)(2,1)}, u32[]{:S(2)}, u32[]{:S(2)}) async-start(bf16[32,64,1024]{2,1,0:T(8,128)(2,1)} %stack.40), calls=%async_computation.1 | async-start | bytes 8388608 | tf_op jit(solution)/shard_map/all_to_all | solution.py:107
  108.9 24.2 %reduce-scatter.9.cloned.1.call-start = ((), (), s32[]{:S(2)}) async-start(), calls=%async_computation.18 | async-start | bytes 655360 | tf_op jit(solution)/shard_map/reduce_scatter | solution.py:26
  174.8 76.2 %all-to-all-start.2 = ((bf16[32,64,1024]{2,1,0:T(8,128)(2,1)}), bf16[32,64,1024]{2,1,0:T(8,128)(2,1)}, u32[]{:S(2)}, u32[]{:S(2)}) async-start(bf16[32,64,1024]{2,1,0:T(8,128)(2,1)} %stack.42), calls=%async_computation.5 | async-start | bytes 8388608 | tf_op jit(solution)/shard_map/all_to_all | solution.py:107
  250.9 17.9 %all-to-all-start.4 = ((f32[4,512,128]{2,1,0:T(8,128)}), f32[4,512,128]{2,1,0:T(8,128)S(1)}, u32[]{:S(2)}, u32[]{:S(2)}) async-start(f32[4,512,128]{2,1,0:T(8,128)} %fusion.7), calls=%async_computation.8 | async-start | bytes 2097152 | tf_op jit(solution)/shard_map/all_to_all | solution.py:37
  268.9 17.9 %all-to-all-start.6 = ((f32[4,512,128]{2,1,0:T(8,128)}), f32[4,512,128]{2,1,0:T(8,128)S(1)}, u32[]{:S(2)}, u32[]{:S(2)}) async-start(f32[4,512,128]{2,1,0:T(8,128)} %fusion.10), calls=%async_computation.10 | async-start | bytes 2097152 | tf_op jit(solution)/shard_map/all_to_all | solution.py:37
  287.6 12.3 %all-to-all-start.5 = ((bf16[4,512,128]{2,1,0:T(8,128)(2,1)}), bf16[4,512,128]{2,1,0:T(8,128)(2,1)S(1)}, u32[]{:S(2)}, u32[]{:S(2)}) async-start(bf16[4,512,128]{2,1,0:T(8,128)(2,1)} %broadcast_in_dim.12), calls=%async_computation.9 | async-start | bytes 1048576 | tf_op jit(solution)/shard_map/all_to_all | solution.py:49
  300.8 12.3 %all-to-all-start.7 = ((bf16[4,512,128]{2,1,0:T(8,128)(2,1)}), bf16[4,512,128]{2,1,0:T(8,128)(2,1)S(1)}, u32[]{:S(2)}, u32[]{:S(2)}) async-start(bf16[4,512,128]{2,1,0:T(8,128)(2,1)} %broadcast_in_dim.13), calls=%async_computation.11 | async-start | bytes 1048576 | tf_op jit(solution)/shard_map/all_to_all | solution.py:49
  395.0 18.7 %all-to-all-start.10 = ((f32[4,512,128]{2,1,0:T(8,128)}), f32[4,512,128]{2,1,0:T(8,128)}, u32[]{:S(2)}, u32[]{:S(2)}) async-start(f32[4,512,128]{2,1,0:T(8,128)} %fusion.12), calls=%async_computation.14 | async-start | bytes 2097152 | tf_op jit(solution)/shard_map/all_to_all | solution.py:37
  413.7 18.8 %all-to-all-start.8 = ((f32[4,512,128]{2,1,0:T(8,128)}), f32[4,512,128]{2,1,0:T(8,128)}, u32[]{:S(2)}, u32[]{:S(2)}) async-start(f32[4,512,128]{2,1,0:T(8,128)} %fusion.14), calls=%async_computation.12 | async-start | bytes 2097152 | tf_op jit(solution)/shard_map/all_to_all | solution.py:37
  433.4 13.0 %all-to-all-start.11 = ((bf16[4,512,128]{2,1,0:T(8,128)(2,1)}), bf16[4,512,128]{2,1,0:T(8,128)(2,1)}, u32[]{:S(2)}, u32[]{:S(2)}) async-start(bf16[4,512,128]{2,1,0:T(8,128)(2,1)} %broadcast_in_dim.15), calls=%async_computation.15 | async-start | bytes 1048576 | tf_op jit(solution)/shard_map/all_to_all | solution.py:49
  447.2 13.0 %all-to-all-start.9 = ((bf16[4,512,128]{2,1,0:T(8,128)(2,1)}), bf16[4,512,128]{2,1,0:T(8,128)(2,1)}, u32[]{:S(2)}, u32[]{:S(2)}) async-start(bf16[4,512,128]{2,1,0:T(8,128)(2,1)} %broadcast_in_dim.14), calls=%async_computation.13 | async-start | bytes 1048576 | tf_op jit(solution)/shard_map/all_to_all | solution.py:49
Sparse Core Ops, SparseCore 0:
  22.3 20.5 reduce-scatter.10
  45.8 20.6 reduce-scatter.6
  69.5 20.0 reduce-scatter.4
  111.8 21.2 reduce-scatter.8
